TPU v7x, 512 devices: a whole 4x8x8 slice. The times are simulated.
512 devices in a mesh: group: 2 (over core), dp: 64 (over y, x, z_hi), mp: 4 (over z_lo).
Axes of the slice: x: 4, y: 8, z: 8 (z_hi: 2, z_lo: 4; z = z_hi * 4 + z_lo), core: 2. Of those that a mesh axis runs over, the one named last changes fastest.
Arguments:
- x_arrive: bfloat16 [256, 256, 1152], P(('group', 'dp')), may hold values from -6 to 6
- cond_first: int32 [128], P(('group', 'dp')), may hold values 0 or 1
- labels: int32 [128], P(('group', 'dp')), may hold values from 0 to 999
- step_ids: int32 [128], P(('group', 'dp')), may hold values from 0 to 999
- guidance: float32 [1], replicated, may hold values from 2 to 6
- time_table: bfloat16 [1000, 1152], P(None, 'mp'), may hold values from -6 to 6
- class_table: bfloat16 [1001, 1152], P(None, 'mp'), may hold values from -6 to 6
- ada_weight: bfloat16 [1152, 6912], P('mp', 'dp'), may hold values from -0.1875 to 0.1875
- final_ada: bfloat16 [1152, 2304], P('mp'), may hold values from -0.1875 to 0.1875
- qkv_weight: bfloat16 [3, 1152, 1152], P(None, 'dp', 'mp'), may hold values from -2 to 2
- proj_weight: bfloat16 [1152, 1152], P('mp', 'dp'), may hold values from -0.1875 to 0.1875
- fc1_weight: bfloat16 [1152, 4608], P('dp', 'mp'), may hold values from -0.1875 to 0.1875
- fc2_weight: bfloat16 [4608, 1152], P('mp', 'dp'), may hold values from -0.09375 to 0.09375
- out_weight: bfloat16 [1152, 16], replicated, may hold values from -0.1875 to 0.1875
Outputs:
- guided: float32 [128, 4096], P(('group', 'dp'), 'mp')
All inputs are finite; a program needn't handle non-finite values. No bound on the sum of `cond_first` on one device may be relied on, other than what follows from the above.
Results may differ from a plain program's by a relative error of at most 0.025.
Values may be sent and summed in bfloat16 or wider, within the bound.
No kernel may reach another device: no remote copies, remote signals or barrier semaphores. Data moves between devices by JAX's collectives and lax.ppermute only.
A program may use at most 64 MiB of HBM per device.

v0:
```python
import jax
import jax.numpy as jnp
from jax import lax
from jax.sharding import Mesh
from jax.sharding import PartitionSpec as P

HEADS = 16
CLASSES = 1000
DP = ("dp_0", "dp_1", "dp_2")
GROUP_DP = ("group", "dp_0", "dp_1", "dp_2")


def from_everyone(x, axis):
    size = lax.axis_size(axis)
    return lax.all_to_all(jnp.broadcast_to(x[None], (size, *x.shape)), axis, 0, 0, tiled=True)


def laid_out(pieces, dim):
    pieces = jnp.moveaxis(pieces, 0, dim)
    shape = pieces.shape
    return pieces.reshape(*shape[:dim], shape[dim] * shape[dim + 1], *shape[dim + 2 :])


def collect(x, axis, dim):
    pieces = from_everyone(x, axis)
    return laid_out(pieces, dim)


def of_everyone(x, axis):
    everything = from_everyone(x, axis)
    return jnp.sum(everything.astype(jnp.float32), axis=0)


def gathered_by_axis(x, axes, dim):
    for axis in reversed(axes):
        x = lax.all_gather(x, axis, axis=dim, tiled=True)
    return x


def cut_along(x, dim, size):
    shape = x.shape
    pieces = x.reshape(*shape[:dim], size, shape[dim] // size, *shape[dim + 1 :])
    return jnp.moveaxis(pieces, dim, 0)


def sum_at_owner(x, axis, dim):
    size = lax.axis_size(axis)
    pieces = lax.all_to_all(cut_along(x, dim, size), axis, 0, 0, tiled=True)
    return jnp.sum(pieces.astype(jnp.float32), axis=0)


def layer_norm(values):
    mean = jnp.mean(values, axis=-1, keepdims=True)
    centred = values - mean
    spread = jnp.mean(centred * centred, axis=-1, keepdims=True)
    return centred * lax.rsqrt(spread + 1e-06)


def on_device(
    x_arrive,
    cond_first,
    labels,
    step_ids,
    guidance,
    time_table,
    class_table,
    ada_weight,
    final_ada,
    qkv_weight,
    proj_weight,
    fc1_weight,
    fc2_weight,
    out_weight,
):
    pair_count = labels.shape[0]
    tokens = x_arrive.shape[1]
    width = x_arrive.shape[2]
    image_count = 2 * pair_count
    row_count = image_count * tokens
    split_rows = x_arrive.reshape(pair_count, 2, tokens, width)
    first = (cond_first == 1)[:, None, None]
    cond_rows = jnp.where(first, split_rows[:, 0], split_rows[:, 1])
    uncond_rows = jnp.where(first, split_rows[:, 1], split_rows[:, 0])
    x_sides = jnp.stack([cond_rows, uncond_rows])
    time_part = jnp.take(time_table, step_ids, axis=0).astype(jnp.float32)
    class_part = jnp.take(class_table, labels, axis=0).astype(jnp.float32)
    null_part = class_table[CLASSES].astype(jnp.float32)[None, :]
    emb_sides = time_part[None] + jnp.stack([class_part, null_part])
    act_sides = jax.nn.silu(emb_sides).astype(jnp.bfloat16)
    images, acts = (x_sides, act_sides)
    images = images.reshape(image_count, tokens, width)
    acts = acts.reshape(image_count, act_sides.shape[2])
    partial_final = jnp.dot(acts, final_ada, preferred_element_type=jnp.float32)
    every_act = collect(acts, DP, 0)
    column_part = jnp.dot(every_act, ada_weight, preferred_element_type=jnp.float32)
    summed, fmods = (
        of_everyone(column_part.astype(jnp.bfloat16), "mp").astype(jnp.float32),
        of_everyone(partial_final.astype(jnp.bfloat16), "mp").astype(jnp.float32),
    )
    mods = lax.all_to_all(
        summed.astype(jnp.bfloat16), DP, split_axis=0, concat_axis=1, tiled=True
    ).astype(summed.dtype)
    shift_a, scale_a, gate_a, shift_m, scale_m, gate_m = jnp.split(mods, 6, axis=1)
    shift_f, scale_f = jnp.split(fmods, 2, axis=1)
    images_f = images.astype(jnp.float32)
    hidden = (layer_norm(images_f) * (1.0 + scale_a[:, None]) + shift_a[:, None]).astype(
        jnp.bfloat16
    )
    hidden = hidden.reshape(row_count, width)
    quarter = qkv_weight.shape[2]
    head_dim = width // HEADS
    local_heads = quarter // head_dim
    columns = hidden
    qkv = jnp.einsum(
        "rd,kdc->krc",
        columns,
        lax.all_gather(qkv_weight, DP, axis=1, tiled=True),
        preferred_element_type=jnp.float32,
    ).astype(jnp.bfloat16)
    query = qkv[0].reshape(image_count, tokens, local_heads, head_dim)
    keys = qkv[1].reshape(image_count, tokens, local_heads, head_dim)
    values = qkv[2].reshape(image_count, tokens, local_heads, head_dim)
    scores = jnp.einsum(
        "bqhe,bkhe->bhqk", query, keys, preferred_element_type=jnp.float32
    ) * head_dim ** (-0.5)
    probs = jax.nn.softmax(scores, axis=-1).astype(jnp.bfloat16)
    mixed = jnp.einsum("bhqk,bkhe->bqhe", probs, values, preferred_element_type=jnp.float32).astype(
        jnp.bfloat16
    )
    mixed = mixed.reshape(row_count, quarter)
    attn_part = jnp.dot(mixed, collect(proj_weight, DP, 1), preferred_element_type=jnp.float32)
    attn = (
        lax.psum(attn_part.astype(jnp.bfloat16), "mp")
        .astype(jnp.float32)
        .reshape(image_count, tokens, width)
    )
    first_sum = images_f + gate_a[:, None] * attn
    hidden_two = (layer_norm(first_sum) * (1.0 + scale_m[:, None]) + shift_m[:, None]).astype(
        jnp.bfloat16
    )
    hidden_two = hidden_two.reshape(row_count, width)
    ff_quarter = fc1_weight.shape[1]
    columns = hidden_two
    up = jnp.dot(columns, gathered_by_axis(fc1_weight, DP, 0), preferred_element_type=jnp.float32)
    gelu_h = (
        jax.nn.gelu(up, approximate=True)
        .astype(jnp.bfloat16)
        .reshape(image_count, tokens, ff_quarter)
    )
    down_full = gathered_by_axis(fc2_weight, DP, 1)
    token_share = tokens // lax.axis_size("mp")
    mlp = sum_at_owner(
        jnp.einsum("btf,fd->tbd", gelu_h, down_full, preferred_element_type=jnp.float32).astype(
            jnp.bfloat16
        ),
        "mp",
        0,
    )
    token_start = lax.axis_index("mp") * token_share
    own_first = lax.dynamic_slice_in_dim(first_sum, token_start, token_share, 1).transpose(1, 0, 2)
    second_sum = own_first + gate_m[None] * mlp
    fin = (layer_norm(second_sum) * (1.0 + scale_f[None]) + shift_f[None]).astype(jnp.bfloat16)
    noise = jnp.einsum("tbd,do->bto", fin, out_weight, preferred_element_type=jnp.float32)
    noise = noise.reshape(2, pair_count, token_share * out_weight.shape[1])
    return noise[1] + guidance[0] * (noise[0] - noise[1])


def solution(mesh):
    torus = Mesh(
        mesh.devices.reshape(mesh.shape["group"], 8, 4, 2, mesh.shape["mp"]),
        ("group", "dp_0", "dp_1", "dp_2", "mp"),
    )
    placed = (
        P(GROUP_DP, None, None),
        P(GROUP_DP),
        P(GROUP_DP),
        P(GROUP_DP),
        P(),
        P(None, "mp"),
        P(None, "mp"),
        P("mp", DP),
        P("mp", None),
        P(None, DP, "mp"),
        P("mp", DP),
        P(DP, "mp"),
        P("mp", DP),
        P(),
    )
    return jax.shard_map(
        on_device, mesh=torus, in_specs=placed, out_specs=P(GROUP_DP, "mp"), check_vma=False
    )
```

profile of v0, /device:TPU:4, one launch (start us, length us, event | category | flops | bytes accessed | tf_op | source)
XLA Modules:
  0.0 341.8 jit_solution(6708045404015547400)
XLA Ops:
  13.9 19.2 %all-to-all-start = ((bf16[64,2,288]{2,1,0:T(2,128)(2,1)}), bf16[64,2,288]{2,1,0:T(2,128)(2,1)S(1)}, u32[]{:S(2)}, u32[]{:S(2)}) async-start(bf16[64,2,288]{2,1,0:T(2,128)(2,1)} %broadcast_in_dim.50), calls=%async_computation | async-start | bytes 196608 | tf_op jit(solution)/shard_map/all_to_all | solution.py:15
  33.8 12.4 %all-to-all-done = bf16[64,2,288]{2,1,0:T(2,128)(2,1)S(1)} async-done(((bf16[64,2,288]{2,1,0:T(2,128)(2,1)}), bf16[64,2,288]{2,1,0:T(2,128)(2,1)S(1)}, u32[]{:S(2)}, u32[]{:S(2)}) %all-to-all-start) | async-done | bytes 73760 | tf_op jit(solution)/shard_map/all_to_all | solution.py:15
  48.1 4.5 %all-to-all-start.1 = ((bf16[4,128,108]{1,2,0:T(8,128)(2,1)}), bf16[4,128,108]{1,2,0:T(8,128)(2,1)S(1)}, u32[]{:S(2)}, u32[]{:S(2)}) async-start(bf16[4,128,108]{1,2,0:T(8,128)(2,1)} %broadcast_in_dim.84), calls=%async_computation.1 | async-start | bytes 229376 | tf_op jit(solution)/shard_map/all_to_all | solution.py:15
  53.9 4.5 %all-to-all-done.1 = bf16[4,128,108]{1,2,0:T(8,128)(2,1)S(1)} async-done(((bf16[4,128,108]{1,2,0:T(8,128)(2,1)}), bf16[4,128,108]{1,2,0:T(8,128)(2,1)S(1)}, u32[]{:S(2)}, u32[]{:S(2)}) %all-to-all-start.1) | async-done | bytes 110624 | tf_op jit(solution)/shard_map/all_to_all | solution.py:15
  59.2 6.2 %all-to-all-start.2 = ((bf16[64,2,108]{2,1,0:T(2,128)(2,1)}), bf16[64,2,108]{2,1,0:T(2,128)(2,1)S(1)}, u32[]{:S(2)}, u32[]{:S(2)}) async-start(bf16[64,2,108]{2,1,0:T(2,128)(2,1)} %bitcast.7), calls=%async_computation.2 | async-start | bytes 65536 | tf_op jit(solution)/shard_map/all_to_all | solution.py:100
  65.6 12.4 %all-to-all-done.2 = bf16[64,2,108]{2,1,0:T(2,128)(2,1)S(1)} async-done(((bf16[64,2,108]{2,1,0:T(2,128)(2,1)}), bf16[64,2,108]{2,1,0:T(2,128)(2,1)S(1)}, u32[]{:S(2)}, u32[]{:S(2)}) %all-to-all-start.2) | async-done | bytes 27680 | tf_op jit(solution)/shard_map/all_to_all | solution.py:100
  79.1 7.2 %all-to-all-start.3 = ((bf16[64,288,18]{1,2,0:T(8,128)(2,1)}), bf16[64,288,18]{1,2,0:T(8,128)(2,1)}, u32[]{:S(2)}, u32[]{:S(2)}) async-start(bf16[64,288,18]{1,2,0:T(8,128)(2,1)} %broadcast_in_dim.85), calls=%async_computation.3 | async-start | bytes 2359296 | tf_op jit(solution)/shard_map/all_to_all | solution.py:15
  88.8 30.6 %all-to-all-done.3 = bf16[64,288,18]{1,2,0:T(8,128)(2,1)} async-done(((bf16[64,288,18]{1,2,0:T(8,128)(2,1)}), bf16[64,288,18]{1,2,0:T(8,128)(2,1)}, u32[]{:S(2)}, u32[]{:S(2)}) %all-to-all-start.3) | async-done | bytes 663584 | tf_op jit(solution)/shard_map/all_to_all | solution.py:15
  121.0 51.8 %all-gather.8.cloned.1.call-done = bf16[3,1152,288]{2,0,1:T(4,128)(2,1)} async-done(((bf16[3,18,288]{2,0,1:T(4,128)(2,1)}), bf16[3,1152,288]{2,0,1:T(4,128)(2,1)}) %all-gather.8.cloned.1.call-update) | async-done | bytes 1990672 | tf_op jit(solution)/shard_map/all_gather | solution.py:117
  172.8 3.7 %fusion.26 = bf16[3,512,288]{1,2,0:T(8,128)(2,1)S(1)} fusion(bf16[3,1152,288]{2,0,1:T(4,128)(2,1)} %all-gather.8.cloned.1.call-done, bf16[512,1152]{1,0:T(8,128)(2,1)} %fusion.16), kind=kOutput, calls=%fused_computation.41 | convolution fusion | flops 1019658240 | bytes 4055040 | tf_op jit(solution)/shard_map/rd,kdc->krc/dot_general | solution.py:114
  182.8 3.2 fusion.65
  186.0 2.0 fusion.30
  190.4 9.3 %all-gather = bf16[2,18,1152]{2,1,0:T(8,128)(2,1)S(1)} all-gather(bf16[1,18,1152]{2,1,0:T(8,128)(2,1)S(1)} %bitcast.125), channel_id=1, replica_groups=mesh['group'=2,'dp_0'=8,'dp_1'=4,'dp_2'=2,'mp'=4] {'dp_2'}, dimensions={0}, use_global_device_ids=true | all-gather | bytes 124416 | tf_op jit(solution)/shard_map/all_gather | solution.py:36
  199.8 11.3 %all-gather.1 = bf16[4,36,1152]{2,1,0:T(8,128)(2,1)S(1)} all-gather(bf16[1,36,1152]{2,1,0:T(8,128)(2,1)S(1)} %reshape.323), channel_id=1, replica_groups=mesh['group'=2,'dp_0'=8,'dp_1'=4,'dp_2'=2,'mp'=4] {'dp_1'}, dimensions={0}, use_global_device_ids=true | all-gather | bytes 414720 | tf_op jit(solution)/shard_map/all_gather | solution.py:36
  211.9 10.3 %all-gather.2 = bf16[2,18,1152]{2,1,0:T(8,128)(2,1)S(1)} all-gather(bf16[1,18,1152]{2,1,0:T(8,128)(2,1)S(1)} %bitcast.126), channel_id=1, replica_groups=mesh['group'=2,'dp_0'=8,'dp_1'=4,'dp_2'=2,'mp'=4] {'dp_2'}, dimensions={0}, use_global_device_ids=true | all-gather | bytes 124416 | tf_op jit(solution)/shard_map/all_gather | solution.py:36
  222.2 12.4 %all-gather.3 = bf16[4,36,1152]{2,1,0:T(8,128)(2,1)S(1)} all-gather(bf16[1,36,1152]{2,1,0:T(8,128)(2,1)S(1)} %reshape.327), channel_id=1, replica_groups=mesh['group'=2,'dp_0'=8,'dp_1'=4,'dp_2'=2,'mp'=4] {'dp_1'}, dimensions={0}, use_global_device_ids=true | all-gather | bytes 414720 | tf_op jit(solution)/shard_map/all_gather | solution.py:36
  236.5 3.4 %all-to-all-start.5 = ((bf16[4,2,2304]{2,1,0:T(2,128)(2,1)}), bf16[4,2,2304]{2,1,0:T(2,128)(2,1)S(1)}, u32[]{:S(2)}, u32[]{:S(2)}) async-start(bf16[4,2,2304]{2,1,0:T(2,128)(2,1)} %broadcast_in_dim.86), calls=%async_computation.5 | async-start | bytes 73728 | tf_op jit(solution)/shard_map/all_to_all | solution.py:15
  240.0 21.1 %all-reduce.2.cloned.1.call-done = bf16[512,1152]{1,0:T(8,128)(2,1)} async-done(((bf16[512,1152]{1,0:T(8,128)(2,1)}), bf16[512,1152]{1,0:T(8,128)(2,1)}) %all-reduce.2.cloned.1.call-update) | async-done | bytes 1179664 | tf_op jit(solution)/shard_map/psum | solution.py:133
  264.9 2.0 fusion.12
  266.9 4.0 %fusion.11 = bf16[512,1152]{1,0:T(8,128)(2,1)S(1)} fusion(bf16[512,1152]{1,0:T(8,128)(2,1)} %fusion.12, bf16[1152,1152]{1,0:T(8,128)(2,1)} %all-gather.10.cloned.1.call-done), kind=kOutput, calls=%fused_computation.15 | convolution fusion | flops 1364262912 | bytes 5013504 | tf_op jit(solution)/shard_map/dot_general | solution.py:144
  271.0 25.5 %all-gather.12.cloned.1.call-done = bf16[1152,1152]{0,1:T(8,128)(2,1)} async-done(((bf16[1152,144]{0,1:T(8,128)(2,1)}), bf16[1152,1152]{0,1:T(8,128)(2,1)}) %all-gather.12.cloned.1.call-update) | async-done | bytes 2654224 | tf_op jit(solution)/shard_map/all_gather | solution.py:36
  296.4 3.6 %convolution_convert_fusion.1 = bf16[2,256,1152]{2,1,0:T(8,128)(2,1)S(1)} fusion(bf16[2,256,1152]{2,1,0:T(8,128)(2,1)S(1)} %bitcast.131, bf16[1152,1152]{0,1:T(8,128)(2,1)} %all-gather.12.cloned.1.call-done), kind=kOutput, calls=%fused_computation.3 | convolution fusion | flops 1359544320 | bytes 5013504 | tf_op jit(solution)/shard_map/btf,fd->tbd/dot_general | solution.py:153
  301.2 4.8 %all-to-all-start.4 = ((bf16[4,64,2,1152]{3,1,2,0:T(8,128)(2,1)}), bf16[4,64,2,1152]{3,1,2,0:T(8,128)(2,1)S(1)}, u32[]{:S(2)}, u32[]{:S(2)}) async-start(bf16[4,64,2,1152]{3,1,2,0:T(8,128)(2,1)} %copy.113), calls=%async_computation.4 | async-start | bytes 2359296 | tf_op jit(solution)/shard_map/all_to_all | solution.py:48
  306.7 24.8 %all-to-all-done.4 = bf16[4,64,2,1152]{3,1,2,0:T(8,128)(2,1)S(1)} async-done(((bf16[4,64,2,1152]{3,1,2,0:T(8,128)(2,1)}), bf16[4,64,2,1152]{3,1,2,0:T(8,128)(2,1)S(1)}, u32[]{:S(2)}, u32[]{:S(2)}) %all-to-all-start.4) | async-done | bytes 1179680 | tf_op jit(solution)/shard_map/all_to_all | solution.py:48
  (91 shorter events, 33.7 us)
Async XLA Ops:
  7.4 228.2 %copy-start = (bf16[288,2304]{1,0:T(8,128)(2,1)S(1)}, bf16[288,2304]{1,0:T(8,128)(2,1)}, u32[]{:S(2)}) copy-start(bf16[288,2304]{1,0:T(8,128)(2,1)} %param.22) | copy-start | bytes 3981316
  7.4 165.5 %all-gather.8.cloned.1.call-start = ((), (), s32[]{:S(2)}) async-start(), calls=%async_computation.6 | async-start | bytes 3594240 | tf_op jit(solution)/shard_map/all_gather | solution.py:117
  12.7 0.6 copy-start.6
  13.9 64.1 %copy-start.5 = (bf16[288,18]{0,1:T(8,128)(2,1)S(1)}, bf16[288,18]{0,1:T(8,128)(2,1)}, u32[]{:S(2)}) copy-start(bf16[288,18]{0,1:T(8,128)(2,1)} %param.24) | copy-start | bytes 31108
  13.9 32.3 %all-to-all-start = ((bf16[64,2,288]{2,1,0:T(2,128)(2,1)}), bf16[64,2,288]{2,1,0:T(2,128)(2,1)S(1)}, u32[]{:S(2)}, u32[]{:S(2)}) async-start(bf16[64,2,288]{2,1,0:T(2,128)(2,1)} %broadcast_in_dim.50), calls=%async_computation | async-start | bytes 196608 | tf_op jit(solution)/shard_map/all_to_all | solution.py:15
  48.1 10.4 %all-to-all-start.1 = ((bf16[4,128,108]{1,2,0:T(8,128)(2,1)}), bf16[4,128,108]{1,2,0:T(8,128)(2,1)S(1)}, u32[]{:S(2)}, u32[]{:S(2)}) async-start(bf16[4,128,108]{1,2,0:T(8,128)(2,1)} %broadcast_in_dim.84), calls=%async_computation.1 | async-start | bytes 229376 | tf_op jit(solution)/shard_map/all_to_all | solution.py:15
  59.2 18.8 %all-to-all-start.2 = ((bf16[64,2,108]{2,1,0:T(2,128)(2,1)}), bf16[64,2,108]{2,1,0:T(2,128)(2,1)S(1)}, u32[]{:S(2)}, u32[]{:S(2)}) async-start(bf16[64,2,108]{2,1,0:T(2,128)(2,1)} %bitcast.7), calls=%async_computation.2 | async-start | bytes 65536 | tf_op jit(solution)/shard_map/all_to_all | solution.py:100
  79.1 40.3 %all-to-all-start.3 = ((bf16[64,288,18]{1,2,0:T(8,128)(2,1)}), bf16[64,288,18]{1,2,0:T(8,128)(2,1)}, u32[]{:S(2)}, u32[]{:S(2)}) async-start(bf16[64,288,18]{1,2,0:T(8,128)(2,1)} %broadcast_in_dim.85), calls=%async_computation.3 | async-start | bytes 2359296 | tf_op jit(solution)/shard_map/all_to_all | solution.py:15
  86.3 174.8 %all-reduce.2.cloned.1.call-start = ((), (), s32[]{:S(2)}) async-start(), calls=%async_computation.7 | async-start | bytes 2359296 | tf_op jit(solution)/shard_map/psum | solution.py:133
  188.0 2.4 copy-start.3
  188.4 23.6 %copy-start.4 = (bf16[1152,18]{0,1:T(8,128)(2,1)S(1)}, bf16[1152,18]{0,1:T(8,128)(2,1)}, u32[]{:S(2)}) copy-start(bf16[1152,18]{0,1:T(8,128)(2,1)} %param.26) | copy-start | bytes 124420
  190.3 45.2 %copy-start.7 = (bf16[2,288]{1,0:T(2,128)(2,1)S(1)}, bf16[2,288]{1,0:T(2,128)(2,1)}, u32[]{:S(2)}) copy-start(bf16[2,288]{1,0:T(2,128)(2,1)} %copy-done.6) | copy-start | bytes 3460
  190.4 76.6 %all-gather.10.cloned.1.call-start = ((), (), s32[]{:S(2)}) async-start(), calls=%async_computation.8 | async-start | bytes 2985984 | tf_op jit(solution)/shard_map/all_gather | solution.py:36
  211.9 84.6 %all-gather.12.cloned.1.call-start = ((), (), s32[]{:S(2)}) async-start(), calls=%async_computation.9 | async-start | bytes 2985984 | tf_op jit(solution)/shard_map/all_gather | solution.py:36
  236.5 64.7 %all-to-all-start.5 = ((bf16[4,2,2304]{2,1,0:T(2,128)(2,1)}), bf16[4,2,2304]{2,1,0:T(2,128)(2,1)S(1)}, u32[]{:S(2)}, u32[]{:S(2)}) async-start(bf16[4,2,2304]{2,1,0:T(2,128)(2,1)} %broadcast_in_dim.86), calls=%async_computation.5 | async-start | bytes 73728 | tf_op jit(solution)/shard_map/all_to_all | solution.py:15
  262.8 1.4 copy-start.1
  262.8 2.1 copy-start.2
  301.2 30.3 %all-to-all-start.4 = ((bf16[4,64,2,1152]{3,1,2,0:T(8,128)(2,1)}), bf16[4,64,2,1152]{3,1,2,0:T(8,128)(2,1)S(1)}, u32[]{:S(2)}, u32[]{:S(2)}) async-start(bf16[4,64,2,1152]{3,1,2,0:T(8,128)(2,1)} %copy.113), calls=%async_computation.4 | async-start | bytes 2359296 | tf_op jit(solution)/shard_map/all_to_all | solution.py:48
  305.9 27.1 %copy-start.8 = (bf16[1152,16]{0,1:T(8,128)(2,1)S(1)}, bf16[1152,16]{0,1:T(8,128)(2,1)}, u32[]{:S(2)}) copy-start(bf16[1152,16]{0,1:T(8,128)(2,1)} %param.27) | copy-start | bytes 110596
Sparse Core Ops, SparseCore 0:
  12.5 160.2 all-gather.7
  190.5 70.5 all-reduce.1
Sparse Core Ops, SparseCore 1:
  212.0 38.8 all-gather.9
  252.8 43.6 all-gather.11
where the time goes:
time: 343 us; the launch traced here: 342 us
  waiting for transfers between devices  183 us (53%)
  starting transfers between devices  45.4 us (13%)
  blocking collectives  43.3 us (13%)
  local copies, waits for them, and re-layouts  21.6 us (6%)
  matrix products  20.2 us (6%)
  between operations  17.8 us (5%)
  other arithmetic  10.3 us (3%)
    all_gather x1, waiting for transfers between devices, on_device(): lax.all_gather(qkv_weight, DP, axis=1, tiled=True)  51.8 us
    all_to_all x4, waiting for transfers between devices, from_everyone(): lax.all_to_all(jnp.broadcast_to(x[None], (size, *x.shape)), axis, 0, 0, t...  47.6 us
    all_gather x4, blocking collectives, gathered_by_axis(): x = lax.all_gather(x, axis, axis=dim, tiled=True)  43.3 us
    all_to_all x4, starting transfers between devices, from_everyone(): lax.all_to_all(jnp.broadcast_to(x[None], (size, *x.shape)), axis, 0, 0, t...  34.3 us
    all_gather x2, waiting for transfers between devices, gathered_by_axis(): x = lax.all_gather(x, axis, axis=dim, tiled=True)  25.5 us
    all_to_all x1, waiting for transfers between devices, sum_at_owner(): pieces = lax.all_to_all(cut_along(x, dim, size), axis, 0, 0, tiled=True)  24.8 us
    psum x1, waiting for transfers between devices, on_device(): lax.psum(attn_part.astype(jnp.bfloat16), 'mp').astype(jnp.float32)  21.1 us
    all_to_all x1, waiting for transfers between devices, on_device(): lax.all_to_all(summed.astype(jnp.bfloat16), DP, split_axis=0, concat_axis...  12.4 us
  transfers between devices with their start and end apart: 10, of which 8 were waited for; matrix products, arithmetic and copies ran while one was open for 8% of the time, Pallas kernels for 0%

commit v1 on v0

--- a/solution.py
+++ b/solution.py
@@ -114,7 +114,9 @@
     qkv = jnp.einsum(
         "rd,kdc->krc",
         columns,
-        lax.all_gather(qkv_weight, DP, axis=1, tiled=True),
+        jnp.concatenate(
+            lax.all_to_all(jnp.stack([qkv_weight] * lax.axis_size(DP)), DP, 0, 0), axis=1
+        ),
         preferred_element_type=jnp.float32,
     ).astype(jnp.bfloat16)
     query = qkv[0].reshape(image_count, tokens, local_heads, head_dim)

time: 343 us -> 388 us (1.13)
  blocking collectives: 43.3 us -> 142 us
  waiting for transfers between devices: 183 us -> 150 us
  starting transfers between devices: 45.4 us -> 17.2 us
  local copies, waits for them, and re-layouts: 21.6 us -> 29.8 us
    all_to_all x0 -> x4, blocking collectives: none -> 96.9 us  [the longest x3 78.7 us: from_everyone(): lax.all_to_all(jnp.broadcast_to(x[None], (size, *x.shape)), axis, 0, 0, t...]
    all_to_all x1, waiting for transfers between devices: 12.4 us -> 77.5 us  [on_device(): lax.all_to_all(jnp.stack([qkv_weight] * lax.axis_size(DP)), DP, 0, 0)]
    all_gather x1 -> x0, waiting for transfers between devices: 51.8 us -> none  [on_device(): lax.all_gather(qkv_weight, DP, axis=1, tiled=True)]
    all_to_all x4 -> x1, waiting for transfers between devices: 47.6 us -> 0.01 us  [from_everyone(): lax.all_to_all(jnp.broadcast_to(x[None], (size, *x.shape)), axis, 0, 0, t...]
    all_to_all x4 -> x1, starting transfers between devices: 34.3 us -> 4.27 us  [from_everyone(): lax.all_to_all(jnp.broadcast_to(x[None], (size, *x.shape)), axis, 0, 0, t...]
    reshape x0 -> x2, local copies, waits for them, and re-layouts: none -> 9.83 us  [on_device(): jnp.concatenate(lax.all_to_all(jnp.stack([qkv_weight] * lax.axis_size(DP)...]
  transfers between devices with their start and end apart: 10 -> 6, of which waited for: 8 -> 4; matrix products, arithmetic and copies ran while one was open for 8% -> 5% of each run, Pallas kernels for 0% -> 0%
where the time goes in v1:
time: 388 us; the launch traced here: 386 us
  waiting for transfers between devices  150 us (39%)
  blocking collectives  142 us (37%)
  local copies, waits for them, and re-layouts  29.8 us (8%)
  matrix products  19.9 us (5%)
  between operations  17.9 us (5%)
  starting transfers between devices  17.2 us (4%)
  other arithmetic  10.1 us (3%)
    all_to_all x3, blocking collectives, from_everyone(): lax.all_to_all(jnp.broadcast_to(x[None], (size, *x.shape)), axis, 0, 0, t...  78.7 us
    all_to_all x1, waiting for transfers between devices, on_device(): lax.all_to_all(jnp.stack([qkv_weight] * lax.axis_size(DP)), DP, 0, 0)  77.5 us
    all_gather x4, blocking collectives, gathered_by_axis(): x = lax.all_gather(x, axis, axis=dim, tiled=True)  44.9 us
    all_gather x2, waiting for transfers between devices, gathered_by_axis(): x = lax.all_gather(x, axis, axis=dim, tiled=True)  26.3 us
    all_to_all x1, waiting for transfers between devices, sum_at_owner(): pieces = lax.all_to_all(cut_along(x, dim, size), axis, 0, 0, tiled=True)  24.8 us
    psum x1, waiting for transfers between devices, on_device(): lax.psum(attn_part.astype(jnp.bfloat16), 'mp').astype(jnp.float32)  21 us
    all_to_all x1, blocking collectives, on_device(): lax.all_to_all(summed.astype(jnp.bfloat16), DP, split_axis=0, concat_axis...  18.2 us
    reshape x2, local copies, waits for them, and re-layouts, on_device(): jnp.concatenate(lax.all_to_all(jnp.stack([qkv_weight] * lax.axis_size(DP)...  9.83 us
  transfers between devices with their start and end apart: 6, of which 4 were waited for; matrix products, arithmetic and copies ran while one was open for 5% of the time, Pallas kernels for 0%

profile of v1, /device:TPU:4, one launch (start us, length us, event | category | flops | bytes accessed | tf_op | source)
XLA Modules:
  0.0 386.3 jit_solution(8923832303763434914)
XLA Ops:
  11.8 32.0 %all_to_all.43 = bf16[64,2,288]{2,1,0:T(2,128)(2,1)S(1)} all-to-all(bf16[64,2,288]{2,1,0:T(2,128)(2,1)S(1)} %broadcast_in_dim.50), channel_id=1, replica_groups=mesh['group'=2,'dp_0'=8,'dp_1'=4,'dp_2'=2,'mp'=4] {'dp_0','dp_1','dp_2'}, dimensions={0} | all-to-all | bytes 147456 | tf_op jit(solution)/shard_map/all_to_all | solution.py:15
  45.0 10.2 %all_to_all.44 = bf16[4,128,108]{1,2,0:T(8,128)(2,1)S(1)} all-to-all(bf16[4,128,108]{1,2,0:T(8,128)(2,1)S(1)} %broadcast_in_dim.84), channel_id=1, replica_groups=mesh['group'=2,'dp_0'=8,'dp_1'=4,'dp_2'=2,'mp'=4] {'mp'}, dimensions={0} | all-to-all | bytes 221184 | tf_op jit(solution)/shard_map/all_to_all | solution.py:15
  55.3 18.2 %all_to_all.45 = bf16[64,2,108]{2,1,0:T(2,128)(2,1)S(1)} all-to-all(bf16[64,2,108]{2,1,0:T(2,128)(2,1)S(1)} %bitcast.116), channel_id=1, replica_groups=mesh['group'=2,'dp_0'=8,'dp_1'=4,'dp_2'=2,'mp'=4] {'dp_0','dp_1','dp_2'}, dimensions={0} | all-to-all | bytes 55296 | tf_op jit(solution)/shard_map/all_to_all | solution.py:100
  74.3 36.5 %all_to_all.46 = bf16[64,288,18]{1,2,0:T(8,128)(2,1)} all-to-all(bf16[64,288,18]{1,2,0:T(8,128)(2,1)S(1)} %broadcast_in_dim.85), channel_id=1, replica_groups=mesh['group'=2,'dp_0'=8,'dp_1'=4,'dp_2'=2,'mp'=4] {'dp_0','dp_1','dp_2'}, dimensions={0} | all-to-all | bytes 1327104 | tf_op jit(solution)/shard_map/all_to_all | solution.py:15
  110.9 2.1 stack.11
  113.0 7.8 %all-to-all-start.3 = ((bf16[64,3,18,288]{3,2,1,0:T(8,128)(2,1)}), bf16[64,3,18,288]{3,2,1,0:T(8,128)(2,1)}, u32[]{:S(2)}, u32[]{:S(2)}) async-start(bf16[64,3,18,288]{3,2,1,0:T(8,128)(2,1)} %stack.11), calls=%async_computation.3 | async-start | bytes 7077888 | tf_op jit(solution)/shard_map/all_to_all | solution.py:118
  126.9 77.5 %all-to-all-done.3 = bf16[64,3,18,288]{3,2,1,0:T(8,128)(2,1)} async-done(((bf16[64,3,18,288]{3,2,1,0:T(8,128)(2,1)}), bf16[64,3,18,288]{3,2,1,0:T(8,128)(2,1)}, u32[]{:S(2)}, u32[]{:S(2)}) %all-to-all-start.3) | async-done | bytes 1990688 | tf_op jit(solution)/shard_map/all_to_all | solution.py:118
  204.4 4.2 %copy.109 = bf16[3,64,18,288]{3,2,1,0:T(8,128)(2,1)} copy(bf16[3,64,18,288]{3,2,0,1:T(8,128)(2,1)} %bitcast.11) | data formatting | bytes 3981312 | tf_op jit(solution)/shard_map/reshape | solution.py:117
  208.6 5.7 %reshape.324 = bf16[3,1152,288]{2,1,0:T(8,128)(2,1)} reshape(bf16[3,64,18,288]{3,2,1,0:T(8,128)(2,1)} %copy.109) | data formatting | bytes 3981312 | tf_op jit(solution)/shard_map/reshape | solution.py:117
  214.3 3.5 fusion.21
  224.0 3.2 fusion.55
  227.2 2.0 fusion.22
  231.8 8.7 %all-gather = bf16[2,18,1152]{2,1,0:T(8,128)(2,1)S(1)} all-gather(bf16[1,18,1152]{2,1,0:T(8,128)(2,1)S(1)} %bitcast.117), channel_id=1, replica_groups=mesh['group'=2,'dp_0'=8,'dp_1'=4,'dp_2'=2,'mp'=4] {'dp_2'}, dimensions={0}, use_global_device_ids=true | all-gather | bytes 124416 | tf_op jit(solution)/shard_map/all_gather | solution.py:36
  240.6 13.4 %all-gather.1 = bf16[4,36,1152]{2,1,0:T(8,128)(2,1)S(1)} all-gather(bf16[1,36,1152]{2,1,0:T(8,128)(2,1)S(1)} %reshape.387), channel_id=1, replica_groups=mesh['group'=2,'dp_0'=8,'dp_1'=4,'dp_2'=2,'mp'=4] {'dp_1'}, dimensions={0}, use_global_device_ids=true | all-gather | bytes 414720 | tf_op jit(solution)/shard_map/all_gather | solution.py:36
  254.9 10.3 %all-gather.2 = bf16[2,18,1152]{2,1,0:T(8,128)(2,1)S(1)} all-gather(bf16[1,18,1152]{2,1,0:T(8,128)(2,1)S(1)} %bitcast.118), channel_id=1, replica_groups=mesh['group'=2,'dp_0'=8,'dp_1'=4,'dp_2'=2,'mp'=4] {'dp_2'}, dimensions={0}, use_global_device_ids=true | all-gather | bytes 124416 | tf_op jit(solution)/shard_map/all_gather | solution.py:36
  265.2 12.4 %all-gather.3 = bf16[4,36,1152]{2,1,0:T(8,128)(2,1)S(1)} all-gather(bf16[1,36,1152]{2,1,0:T(8,128)(2,1)S(1)} %reshape.391), channel_id=1, replica_groups=mesh['group'=2,'dp_0'=8,'dp_1'=4,'dp_2'=2,'mp'=4] {'dp_1'}, dimensions={0}, use_global_device_ids=true | all-gather | bytes 414720 | tf_op jit(solution)/shard_map/all_gather | solution.py:36
  279.4 4.3 %all-to-all-start.6 = ((bf16[4,2,2304]{2,1,0:T(2,128)(2,1)}), bf16[4,2,2304]{2,1,0:T(2,128)(2,1)S(1)}, u32[]{:S(2)}, u32[]{:S(2)}) async-start(bf16[4,2,2304]{2,1,0:T(2,128)(2,1)} %broadcast_in_dim.86), calls=%async_computation.6 | async-start | bytes 73728 | tf_op jit(solution)/shard_map/all_to_all | solution.py:15
  283.7 21.0 %all-reduce.2.cloned.1.call-done = bf16[512,1152]{1,0:T(8,128)(2,1)} async-done(((bf16[512,1152]{1,0:T(8,128)(2,1)}), bf16[512,1152]{1,0:T(8,128)(2,1)}) %all-reduce.2.cloned.1.call-update) | async-done | bytes 1179664 | tf_op jit(solution)/shard_map/psum | solution.py:135
  308.6 2.0 fusion.10
  310.6 4.0 %fusion.9 = bf16[512,1152]{1,0:T(8,128)(2,1)S(1)} fusion(bf16[512,1152]{1,0:T(8,128)(2,1)} %fusion.10, bf16[1152,1152]{1,0:T(8,128)(2,1)} %all-gather.7.cloned.1.call-done), kind=kOutput, calls=%fused_computation.13 | convolution fusion | flops 1364262912 | bytes 5013504 | tf_op jit(solution)/shard_map/dot_general | solution.py:146
  314.6 26.3 %all-gather.9.cloned.1.call-done = bf16[1152,1152]{0,1:T(8,128)(2,1)} async-done(((bf16[1152,144]{0,1:T(8,128)(2,1)}), bf16[1152,1152]{0,1:T(8,128)(2,1)}) %all-gather.9.cloned.1.call-update) | async-done | bytes 2654224 | tf_op jit(solution)/shard_map/all_gather | solution.py:36
  340.9 3.6 convolution_convert_fusion.1
  345.6 4.8 %all-to-all-start.5 = ((bf16[4,64,2,1152]{3,1,2,0:T(8,128)(2,1)}), bf16[4,64,2,1152]{3,1,2,0:T(8,128)(2,1)S(1)}, u32[]{:S(2)}, u32[]{:S(2)}) async-start(bf16[4,64,2,1152]{3,1,2,0:T(8,128)(2,1)} %copy.116), calls=%async_computation.5 | async-start | bytes 2359296 | tf_op jit(solution)/shard_map/all_to_all | solution.py:48
  351.2 24.8 %all-to-all-done.5 = bf16[4,64,2,1152]{3,1,2,0:T(8,128)(2,1)S(1)} async-done(((bf16[4,64,2,1152]{3,1,2,0:T(8,128)(2,1)}), bf16[4,64,2,1152]{3,1,2,0:T(8,128)(2,1)S(1)}, u32[]{:S(2)}, u32[]{:S(2)}) %all-to-all-start.5) | async-done | bytes 1179680 | tf_op jit(solution)/shard_map/all_to_all | solution.py:48
  (86 shorter events, 29.9 us)
Async XLA Ops:
  7.4 271.1 %copy-start = (bf16[288,2304]{1,0:T(8,128)(2,1)S(1)}, bf16[288,2304]{1,0:T(8,128)(2,1)}, u32[]{:S(2)}) copy-start(bf16[288,2304]{1,0:T(8,128)(2,1)} %param.22) | copy-start | bytes 3981316
  11.2 0.6 copy-start.6
  11.8 99.1 %copy-start.5 = (bf16[3,18,288]{2,1,0:T(8,128)(2,1)S(1)}, bf16[3,18,288]{2,1,0:T(8,128)(2,1)}, u32[]{:S(2)}) copy-start(bf16[3,18,288]{2,1,0:T(8,128)(2,1)} %param.23) | copy-start | bytes 93316
  113.0 91.5 %all-to-all-start.3 = ((bf16[64,3,18,288]{3,2,1,0:T(8,128)(2,1)}), bf16[64,3,18,288]{3,2,1,0:T(8,128)(2,1)}, u32[]{:S(2)}, u32[]{:S(2)}) async-start(bf16[64,3,18,288]{3,2,1,0:T(8,128)(2,1)} %stack.11), calls=%async_computation.3 | async-start | bytes 7077888 | tf_op jit(solution)/shard_map/all_to_all | solution.py:118
  120.8 183.9 %all-reduce.2.cloned.1.call-start = ((), (), s32[]{:S(2)}) async-start(), calls=%async_computation.7 | async-start | bytes 2359296 | tf_op jit(solution)/shard_map/psum | solution.py:135
  229.2 2.6 copy-start.3
  229.6 25.2 %copy-start.4 = (bf16[1152,18]{0,1:T(8,128)(2,1)S(1)}, bf16[1152,18]{0,1:T(8,128)(2,1)}, u32[]{:S(2)}) copy-start(bf16[1152,18]{0,1:T(8,128)(2,1)} %param.26) | copy-start | bytes 124420
  231.6 47.0 %copy-start.7 = (bf16[2,288]{1,0:T(2,128)(2,1)S(1)}, bf16[2,288]{1,0:T(2,128)(2,1)}, u32[]{:S(2)}) copy-start(bf16[2,288]{1,0:T(2,128)(2,1)} %copy-done.6) | copy-start | bytes 3460
  231.6 79.0 %all-gather.7.cloned.1.call-start = ((), (), s32[]{:S(2)}) async-start(), calls=%async_computation.8 | async-start | bytes 2985984 | tf_op jit(solution)/shard_map/all_gather | solution.py:36
  254.8 86.1 %all-gather.9.cloned.1.call-start = ((), (), s32[]{:S(2)}) async-start(), calls=%async_computation.9 | async-start | bytes 2985984 | tf_op jit(solution)/shard_map/all_gather | solution.py:36
  279.4 66.2 %all-to-all-start.6 = ((bf16[4,2,2304]{2,1,0:T(2,128)(2,1)}), bf16[4,2,2304]{2,1,0:T(2,128)(2,1)S(1)}, u32[]{:S(2)}, u32[]{:S(2)}) async-start(bf16[4,2,2304]{2,1,0:T(2,128)(2,1)} %broadcast_in_dim.86), calls=%async_computation.6 | async-start | bytes 73728 | tf_op jit(solution)/shard_map/all_to_all | solution.py:15
  306.4 1.5 copy-start.1
  306.4 2.1 copy-start.2
  345.6 30.3 %all-to-all-start.5 = ((bf16[4,64,2,1152]{3,1,2,0:T(8,128)(2,1)}), bf16[4,64,2,1152]{3,1,2,0:T(8,128)(2,1)S(1)}, u32[]{:S(2)}, u32[]{:S(2)}) async-start(bf16[4,64,2,1152]{3,1,2,0:T(8,128)(2,1)} %copy.116), calls=%async_computation.5 | async-start | bytes 2359296 | tf_op jit(solution)/shard_map/all_to_all | solution.py:48
  350.4 27.1 %copy-start.8 = (bf16[1152,16]{0,1:T(8,128)(2,1)S(1)}, bf16[1152,16]{0,1:T(8,128)(2,1)}, u32[]{:S(2)}) copy-start(bf16[1152,16]{0,1:T(8,128)(2,1)} %param.27) | copy-start | bytes 110596
Sparse Core Ops, SparseCore 0:
  231.7 72.9 all-reduce.1
Sparse Core Ops, SparseCore 1:
  254.9 40.3 all-gather.6
  297.1 43.7 all-gather.8
